TPU v7x, 64 devices: a 2x2x8 block of a 4x4x8 slice. The times are simulated.
64 devices in a mesh: dp: 4 (over x, y), sp: 16 (over z, core).
Axes of the slice: x: 2, y: 2, z: 8, core: 2. Of those that a mesh axis runs over, the one named last changes fastest.
The devices are a block of a 4x4x8 slice.
Arguments:
- images: float32 [32, 256, 256, 3], P('dp', 'sp'), parts along dimension 0
- w_patch: bfloat16 [16, 16, 3, 768], replicated
- b_patch: float32 [768], replicated
- pos_embed: bfloat16 [256, 768], P('sp')
- ln1_gain: float32 [768], replicated
- ln1_bias: float32 [768], replicated
- w_qkv: bfloat16 [768, 3, 12, 64], replicated
- b_qkv: float32 [3, 12, 64], replicated
- w_out: bfloat16 [12, 64, 768], replicated
- b_out: float32 [768], replicated
- ln2_gain: float32 [768], replicated
- ln2_bias: float32 [768], replicated
- w_fc1: bfloat16 [768, 3072], replicated
- b_fc1: float32 [3072], replicated
- w_fc2: bfloat16 [3072, 768], replicated
- b_fc2: float32 [768], replicated
Outputs:
- output: bfloat16 [32, 256, 768], P('dp', 'sp'), parts along dimension 0
There are 4 independent parts. A program takes and returns all parts, laid end to end along the dimension named above; an argument that names none is the same for every part.
All inputs are finite; a program needn't handle non-finite values.
Results may differ from a plain program's by a relative error of at most 0.0126143.
Values are sent between devices in bfloat16 or wider.
A program may use at most 768 MiB of HBM per device.

v0:
```python
import math
import jax
import jax.numpy as jnp
from jax import lax
from jax.sharding import PartitionSpec as P

LN_EPS = 1e-6


def layer_norm(x_in, ln_gain, ln_bias):
    row_mean = jnp.mean(x_in, axis=-1, keepdims=True)
    centered = x_in - row_mean
    variance = jnp.mean(centered * centered, axis=-1, keepdims=True)
    return centered * lax.rsqrt(variance + LN_EPS) * ln_gain + ln_bias


def embed_tokens(images, w_patch, b_patch, pos_embed):
    num_images, num_rows, num_cols, channels = images.shape
    patch_len = w_patch.shape[0]
    grid_rows = num_rows // patch_len
    grid_cols = num_cols // patch_len
    pixels = images.astype(jnp.bfloat16).reshape(num_images, grid_rows, patch_len, grid_cols, patch_len, channels)
    patch_embed = jnp.einsum('bypxqc,pqcd->byxd', pixels, w_patch, preferred_element_type=jnp.float32)
    patch_embed = patch_embed.reshape(num_images, grid_rows * grid_cols, w_patch.shape[3])
    return (patch_embed + b_patch + pos_embed.astype(jnp.float32)).astype(jnp.bfloat16)


def attend(queries, keys_all, values_all):
    num_images, n_query, num_heads, head_dim = queries.shape
    tile_len = math.gcd(n_query, 128)
    score_scale = head_dim ** -0.5

    def one_image(operands):
        q_img, k_img, v_img = operands

        def one_group(q_group):
            scores = jnp.einsum('qhe,khe->hqk', q_group, k_img, preferred_element_type=jnp.float32) * score_scale
            att_weights = jax.nn.softmax(scores, axis=-1).astype(jnp.bfloat16)
            return jnp.einsum('hqk,khe->qhe', att_weights, v_img, preferred_element_type=jnp.float32).astype(jnp.bfloat16)

        grouped = lax.map(one_group, q_img.reshape(n_query // tile_len, tile_len, num_heads, head_dim))
        return grouped.reshape(n_query, num_heads, head_dim)

    return lax.map(one_image, (queries, keys_all, values_all))


def finish_layer(x_zero, attended, w_out, b_out, ln2_gain, ln2_bias, w_fc1, b_fc1, w_fc2, b_fc2):
    residual = x_zero.astype(jnp.float32) + jnp.einsum('bnhe,hed->bnd', attended, w_out, preferred_element_type=jnp.float32) + b_out
    normed_two = layer_norm(residual, ln2_gain, ln2_bias).astype(jnp.bfloat16)
    hidden = jax.nn.gelu(jnp.einsum('bnd,df->bnf', normed_two, w_fc1, preferred_element_type=jnp.float32) + b_fc1, approximate=True).astype(jnp.bfloat16)
    return (residual + jnp.einsum('bnf,fd->bnd', hidden, w_fc2, preferred_element_type=jnp.float32) + b_fc2).astype(jnp.bfloat16)


def solution(mesh):
    def device_step(images, w_patch, b_patch, pos_embed, ln1_gain, ln1_bias, w_qkv, b_qkv, w_out, b_out, ln2_gain, ln2_bias, w_fc1, b_fc1, w_fc2, b_fc2):
        x_zero = embed_tokens(images, w_patch, b_patch, pos_embed)
        normed = layer_norm(x_zero.astype(jnp.float32), ln1_gain, ln1_bias).astype(jnp.bfloat16)
        qkv_proj = (jnp.einsum('bnd,dthe->bnthe', normed, w_qkv, preferred_element_type=jnp.float32) + b_qkv).astype(jnp.bfloat16)
        key_value = lax.all_gather(qkv_proj[:, :, 1:], 'sp', axis=1, tiled=True)
        attended = attend(qkv_proj[:, :, 0], key_value[:, :, 0], key_value[:, :, 1])
        return finish_layer(x_zero, attended, w_out, b_out, ln2_gain, ln2_bias, w_fc1, b_fc1, w_fc2, b_fc2)

    in_specs = (P('dp', 'sp', None, None), P(), P(), P('sp', None), P(), P(), P(), P(), P(), P(), P(), P(), P(), P(), P(), P())
    return jax.shard_map(device_step, mesh=mesh, in_specs=in_specs, out_specs=P('dp', 'sp', None), check_vma=False)
```

profile of v0, /device:TPU:21, one launch (start us, length us, event | category | flops | bytes accessed | tf_op | source)
XLA Modules:
  0.0 173.2 jit_solution(7767456940271025073)
XLA Ops:
  6.6 1.5 convert_element_type.40
  8.1 1.7 convert_element_type.39
  9.8 2.9 %reshape.46 = bf16[8,16,16,16,3]{3,2,1,4,0:T(8,128)(2,1)} reshape(bf16[8,16,256,3]{2,1,3,0:T(8,128)(2,1)} %convert_element_type.39) | data formatting | bytes 393216 | tf_op jit(solution)/shard_map/reshape
  12.7 2.9 %fusion.109 = (f32[8,16]{1,0:T(8,128)S(1)}, f32[8,16,768]{2,1,0:T(8,128)S(1)}) fusion(f32[16,768]{1,0:T(8,128)} %convert_element_type.40, f32[768]{0:T(1024)S(1)} %copy-done.5, bf16[8,16,16,16,3]{3,2,1,4,0:T(8,128)(2,1)} %reshape.46, bf16[16,16,3,768]{3,1,2,0:T(8,128)(2,1)} %param.19), kind=kOutput, calls=%fused_computation.78 | convolution fusion | flops 151486336 | bytes 1822208 | tf_op jit(solution)/shard_map/bypxqc,pqcd->byxd/dot_general | solution.py:23
  15.9 1.9 %add_convert_fusion = bf16[8,16,3,12,64]{4,1,3,2,0:T(8,128)(2,1)S(1)} fusion(bf16[768,3,12,64]{0,3,2,1:T(8,128)(2,1)S(1)} %copy-done, f32[3,12,64]{2,1,0:T(8,128)S(1)} %copy-done.4, f32[8,16,768]{2,1,0:T(8,128)S(1)} %get-tuple-element.66, f32[768]{0:T(1024)S(1)} %copy-done.6, f32[768]{0:T(1024)S(1)} %copy-done.7, f32[8,16]{1,0:T(8,128)S(1)} %add_rsqrt_fusion.1, ...), kind=kOutput, calls=%fused_computation.32 | convolution fusion | flops 454066176 | bytes 4538368 | tf_op jit(solution)/shard_map/bnd,dthe->bnthe/dot_general | solution.py:58
  17.7 1.1 copy-done.1
  18.8 1.0 slice.16
  19.9 1.8 %slice_bitcast_fusion.2 = bf16[8,16,12,64]{3,1,2,0:T(8,128)(2,1)} fusion(bf16[8,16,3,12,64]{4,1,3,2,0:T(8,128)(2,1)} %copy-done.1), kind=kLoop, calls=%fused_computation.55 | loop fusion | bytes 393216 | tf_op jit(solution)/shard_map/squeeze | solution.py:60
  21.7 81.2 %all-gather.2.cloned.1.call-done = bf16[8,256,2,12,64]{4,1,3,2,0:T(8,128)(2,1)} async-done(((bf16[8,16,2,12,64]{4,1,3,2,0:T(8,128)(2,1)}), bf16[8,256,2,12,64]{4,1,3,2,0:T(8,128)(2,1)}) %all-gather.2.cloned.1.call-update) | async-done | bytes 6291472 | tf_op jit(solution)/shard_map/all_gather | solution.py:59
  102.9 12.0 %slice_bitcast_fusion = (bf16[8,256,12,64]{3,1,2,0:T(8,128)(2,1)}, bf16[8,256,12,64]{3,1,2,0:T(8,128)(2,1)}) fusion(bf16[8,256,2,12,64]{4,1,3,2,0:T(8,128)(2,1)} %all-gather.2.cloned.1.call-done), kind=kLoop, calls=%fused_computation.22 | loop fusion | bytes 12582912 | tf_op jit(solution)/shard_map/squeeze | solution.py:60
  115.0 6.7 %copy.19 = bf16[8,256,12,64]{1,3,2,0:T(8,128)(2,1)} copy(bf16[8,256,12,64]{3,1,2,0:T(8,128)(2,1)} %get-tuple-element.63) | data formatting | bytes 6291456 | tf_op jit(solution)/shard_map/while | solution.py:44
  121.7 6.7 %copy.18 = bf16[8,256,12,64]{1,3,2,0:T(8,128)(2,1)} copy(bf16[8,256,12,64]{3,1,2,0:T(8,128)(2,1)} %get-tuple-element.64) | data formatting | bytes 6291456 | tf_op jit(solution)/shard_map/while | solution.py:44
  128.4 28.5 %while.10 = (s32[]{:T(128)}, bf16[8,16,12,64]{3,1,2,0:T(8,128)(2,1)}, bf16[8,256,12,64]{1,3,2,0:T(8,128)(2,1)}, bf16[8,16,12,64]{3,1,2,0:T(8,128)(2,1)}, bf16[8,256,12,64]{1,3,2,0:T(8,128)(2,1)}, /*index=5*/s32[]{:T(128)}) while((s32[]{:T(128)}, bf16[8,16,12,64]{3,1,2,0:T(8,128)(2,1)}, bf16[8,256,12,64]{1,3,2,0:T(8,128)(2,1)}, ...), condition=%wide.region_5.6_spmd, body=%wide.region_2.5_spmd.sunk | while | flops 19231424 | bytes 1331789 | solution.py:44
  128.4 1.4 fusion.126
  129.8 2.2 %fusion.127 = bf16[8,16,12,64]{3,1,2,0:T(8,128)(2,1)} fusion(bf16[8,16,12,64]{3,1,2,0:T(8,128)(2,1)} %get-tuple-element.107, s32[]{:T(128)S(6)} %copy.40, bf16[8,256,12,64]{1,3,2,0:T(8,128)(2,1)} %get-tuple-element.114, f32[12,16]{1,0:T(8,128)S(1)} %fusion.126, bf16[8,256,12,64]{1,3,2,0:T(8,128)(2,1)} %get-tuple-element.116, ...), kind=kOutput, calls=%fused_computation.6.clone.1 | convolution fusion | flops 12792255 | bytes 887552 | tf_op jit(solution)/shard_map/while/body/eval_jaxpr/while/body/eval_jaxpr/hqk,khe->qhe/dot_general | solution.py:39
  132.0 1.4 fusion.126
  133.4 2.2 %fusion.127 = bf16[8,16,12,64]{3,1,2,0:T(8,128)(2,1)} fusion(bf16[8,16,12,64]{3,1,2,0:T(8,128)(2,1)} %get-tuple-element.107, s32[]{:T(128)S(6)} %copy.40, bf16[8,256,12,64]{1,3,2,0:T(8,128)(2,1)} %get-tuple-element.114, f32[12,16]{1,0:T(8,128)S(1)} %fusion.126, bf16[8,256,12,64]{1,3,2,0:T(8,128)(2,1)} %get-tuple-element.116, ...), kind=kOutput, calls=%fused_computation.6.clone.1 | convolution fusion | flops 12792255 | bytes 887552 | tf_op jit(solution)/shard_map/while/body/eval_jaxpr/while/body/eval_jaxpr/hqk,khe->qhe/dot_general | solution.py:39
  135.6 1.4 fusion.126
  136.9 2.2 %fusion.127 = bf16[8,16,12,64]{3,1,2,0:T(8,128)(2,1)} fusion(bf16[8,16,12,64]{3,1,2,0:T(8,128)(2,1)} %get-tuple-element.107, s32[]{:T(128)S(6)} %copy.40, bf16[8,256,12,64]{1,3,2,0:T(8,128)(2,1)} %get-tuple-element.114, f32[12,16]{1,0:T(8,128)S(1)} %fusion.126, bf16[8,256,12,64]{1,3,2,0:T(8,128)(2,1)} %get-tuple-element.116, ...), kind=kOutput, calls=%fused_computation.6.clone.1 | convolution fusion | flops 12792255 | bytes 887552 | tf_op jit(solution)/shard_map/while/body/eval_jaxpr/while/body/eval_jaxpr/hqk,khe->qhe/dot_general | solution.py:39
  139.1 1.4 fusion.126
  140.5 2.2 %fusion.127 = bf16[8,16,12,64]{3,1,2,0:T(8,128)(2,1)} fusion(bf16[8,16,12,64]{3,1,2,0:T(8,128)(2,1)} %get-tuple-element.107, s32[]{:T(128)S(6)} %copy.40, bf16[8,256,12,64]{1,3,2,0:T(8,128)(2,1)} %get-tuple-element.114, f32[12,16]{1,0:T(8,128)S(1)} %fusion.126, bf16[8,256,12,64]{1,3,2,0:T(8,128)(2,1)} %get-tuple-element.116, ...), kind=kOutput, calls=%fused_computation.6.clone.1 | convolution fusion | flops 12792255 | bytes 887552 | tf_op jit(solution)/shard_map/while/body/eval_jaxpr/while/body/eval_jaxpr/hqk,khe->qhe/dot_general | solution.py:39
  142.7 1.4 fusion.126
  144.1 2.2 %fusion.127 = bf16[8,16,12,64]{3,1,2,0:T(8,128)(2,1)} fusion(bf16[8,16,12,64]{3,1,2,0:T(8,128)(2,1)} %get-tuple-element.107, s32[]{:T(128)S(6)} %copy.40, bf16[8,256,12,64]{1,3,2,0:T(8,128)(2,1)} %get-tuple-element.114, f32[12,16]{1,0:T(8,128)S(1)} %fusion.126, bf16[8,256,12,64]{1,3,2,0:T(8,128)(2,1)} %get-tuple-element.116, ...), kind=kOutput, calls=%fused_computation.6.clone.1 | convolution fusion | flops 12792255 | bytes 887552 | tf_op jit(solution)/shard_map/while/body/eval_jaxpr/while/body/eval_jaxpr/hqk,khe->qhe/dot_general | solution.py:39
  146.2 1.4 fusion.126
  147.6 2.2 %fusion.127 = bf16[8,16,12,64]{3,1,2,0:T(8,128)(2,1)} fusion(bf16[8,16,12,64]{3,1,2,0:T(8,128)(2,1)} %get-tuple-element.107, s32[]{:T(128)S(6)} %copy.40, bf16[8,256,12,64]{1,3,2,0:T(8,128)(2,1)} %get-tuple-element.114, f32[12,16]{1,0:T(8,128)S(1)} %fusion.126, bf16[8,256,12,64]{1,3,2,0:T(8,128)(2,1)} %get-tuple-element.116, ...), kind=kOutput, calls=%fused_computation.6.clone.1 | convolution fusion | flops 12792255 | bytes 887552 | tf_op jit(solution)/shard_map/while/body/eval_jaxpr/while/body/eval_jaxpr/hqk,khe->qhe/dot_general | solution.py:39
  149.8 1.4 fusion.126
  151.2 2.2 %fusion.127 = bf16[8,16,12,64]{3,1,2,0:T(8,128)(2,1)} fusion(bf16[8,16,12,64]{3,1,2,0:T(8,128)(2,1)} %get-tuple-element.107, s32[]{:T(128)S(6)} %copy.40, bf16[8,256,12,64]{1,3,2,0:T(8,128)(2,1)} %get-tuple-element.114, f32[12,16]{1,0:T(8,128)S(1)} %fusion.126, bf16[8,256,12,64]{1,3,2,0:T(8,128)(2,1)} %get-tuple-element.116, ...), kind=kOutput, calls=%fused_computation.6.clone.1 | convolution fusion | flops 12792255 | bytes 887552 | tf_op jit(solution)/shard_map/while/body/eval_jaxpr/while/body/eval_jaxpr/hqk,khe->qhe/dot_general | solution.py:39
  153.4 1.4 fusion.126
  154.7 2.2 %fusion.127 = bf16[8,16,12,64]{3,1,2,0:T(8,128)(2,1)} fusion(bf16[8,16,12,64]{3,1,2,0:T(8,128)(2,1)} %get-tuple-element.107, s32[]{:T(128)S(6)} %copy.40, bf16[8,256,12,64]{1,3,2,0:T(8,128)(2,1)} %get-tuple-element.114, f32[12,16]{1,0:T(8,128)S(1)} %fusion.126, bf16[8,256,12,64]{1,3,2,0:T(8,128)(2,1)} %get-tuple-element.116, ...), kind=kOutput, calls=%fused_computation.6.clone.1 | convolution fusion | flops 12792255 | bytes 887552 | tf_op jit(solution)/shard_map/while/body/eval_jaxpr/while/body/eval_jaxpr/hqk,khe->qhe/dot_general | solution.py:39
  156.9 1.9 %fusion.110 = (f32[8,16]{1,0:T(8,128)S(1)}, f32[8,16,768]{2,1,0:T(8,128)S(1)}) fusion(f32[768]{0:T(1024)S(1)} %copy-done.8, f32[8,16,768]{2,1,0:T(8,128)} %copy-done.2, bf16[8,16,12,64]{3,1,2,0:T(8,128)(2,1)} %get-tuple-element.47, bf16[12,64,768]{2,1,0:T(8,128)(2,1)} %param.26), kind=kOutput, calls=%fused_computation.79 | convolution fusion | flops 151289728 | bytes 2166272 | tf_op jit(solution)/shard_map/bnhe,hed->bnd/dot_general | solution.py:48
  158.9 0.7 copy-done.3
  159.8 6.5 %fusion.81 = bf16[8,16,768]{2,1,0:T(8,128)(2,1)} fusion(f32[8,16,768]{2,1,0:T(8,128)} %copy-done.3, bf16[3072,768]{1,0:T(8,128)(2,1)} %param.32, bf16[768,3072]{1,0:T(8,128)(2,1)} %param.30, f32[3072]{0:T(1024)} %param.31, f32[768]{0:T(1024)S(1)} %copy-done.9, f32[768]{0:T(1024)S(1)} %copy-done.10, f32[768]{0:T(1024)} %param.28, ...), kind=kOutput, calls=%fused_computation.54 | convolution fusion | flops 1212678144 | bytes 10049536 | tf_op jit(solution)/shard_map/bnf,fd->bnd/dot_general | solution.py:51
  (29 shorter events, 0.5 us)
Async XLA Ops:
  6.5 9.3 %copy-start = (bf16[768,3,12,64]{0,3,2,1:T(8,128)(2,1)S(1)}, bf16[768,3,12,64]{0,3,2,1:T(8,128)(2,1)}, u32[]{:S(2)}) copy-start(bf16[768,3,12,64]{0,3,2,1:T(8,128)(2,1)} %param.24) | copy-start | bytes 10616836
  6.6 6.2 %copy-start.5 = (f32[768]{0:T(1024)S(1)}, f32[768]{0:T(1024)}, u32[]{:S(2)}) copy-start(f32[768]{0:T(1024)} %param.20) | copy-start | bytes 9220
  6.6 96.4 %all-gather.2.cloned.1.call-start = ((), (), s32[]{:S(2)}) async-start(), calls=%async_computation | async-start | bytes 13369344 | tf_op jit(solution)/shard_map/all_gather | solution.py:59
  12.7 3.1 %copy-start.4 = (f32[3,12,64]{2,1,0:T(8,128)S(1)}, f32[3,12,64]{2,1,0:T(8,128)}, u32[]{:S(2)}) copy-start(f32[3,12,64]{2,1,0:T(8,128)} %param.25) | copy-start | bytes 27652
  12.7 3.1 %copy-start.6 = (f32[768]{0:T(1024)S(1)}, f32[768]{0:T(1024)}, u32[]{:S(2)}) copy-start(f32[768]{0:T(1024)} %param.23) | copy-start | bytes 9220
  12.7 3.1 %copy-start.7 = (f32[768]{0:T(1024)S(1)}, f32[768]{0:T(1024)}, u32[]{:S(2)}) copy-start(f32[768]{0:T(1024)} %param.22) | copy-start | bytes 9220
  15.6 2.1 %copy-start.2 = (f32[8,16,768]{2,1,0:T(8,128)}, f32[8,16,768]{2,1,0:T(8,128)S(1)}, u32[]{:S(2)}) copy-start(f32[8,16,768]{2,1,0:T(8,128)S(1)} %get-tuple-element.66) | copy-start | bytes 1179652
  17.7 1.1 copy-start.1
  128.4 28.5 %copy-start.8 = (f32[768]{0:T(1024)S(1)}, f32[768]{0:T(1024)}, u32[]{:S(2)}) copy-start(f32[768]{0:T(1024)} %param.27) | copy-start | bytes 9220
  156.9 2.9 %copy-start.9 = (f32[768]{0:T(1024)S(1)}, f32[768]{0:T(1024)}, u32[]{:S(2)}) copy-start(f32[768]{0:T(1024)} %param.33) | copy-start | bytes 9220
  156.9 2.9 %copy-start.10 = (f32[768]{0:T(1024)S(1)}, f32[768]{0:T(1024)}, u32[]{:S(2)}) copy-start(f32[768]{0:T(1024)} %param.29) | copy-start | bytes 9220
  158.9 0.7 copy-start.3
Sparse Core Ops, SparseCore 0:
  20.0 82.8 all-gather.1
where the time goes:
time: 174 us; the launch traced here: 173 us
  waiting for transfers between devices  81.3 us (47%)
  matrix products  41.6 us (24%)
  local copies, waits for them, and re-layouts  33.1 us (19%)
  between operations  13.6 us (8%)
  other arithmetic  3.58 us (2%)
    all_gather x1, waiting for transfers between devices, device_step(): key_value = lax.all_gather(qkv_proj[:, :, 1:], 'sp', axis=1, tiled=True)  81.2 us
    dot_general x8, matrix products, one_group(): jnp.einsum('hqk,khe->qhe', att_weights, v_img, preferred_element_type=jnp...  17.6 us
    squeeze x2, local copies, waits for them, and re-layouts, device_step(): attended = attend(qkv_proj[:, :, 0], key_value[:, :, 0], key_value[:, :, 1])  13.8 us
    while x2, local copies, waits for them, and re-layouts, attend(): return lax.map(one_image, (queries, keys_all, values_all))  13.5 us
    sub x8, matrix products, one_group(): att_weights = jax.nn.softmax(scores, axis=-1).astype(jnp.bfloat16)  10.8 us
    dot_general x1, matrix products, finish_layer(): jnp.einsum('bnf,fd->bnd', hidden, w_fc2, preferred_element_type=jnp.float32)  6.5 us
  transfers between devices with their start and end apart: 1, of which 1 were waited for; matrix products, arithmetic and copies ran while one was open for 1% of the time, Pallas kernels for 0%

commit v1 on v0

v1 whole, which is shorter than its diff:
```python
import functools
import math

import jax
import jax.numpy as jnp
from jax import lax
from jax.experimental import pallas as pl
from jax.experimental.pallas import tpu as pltpu
from jax.sharding import PartitionSpec as P

MESH = pl.DeviceIdType.MESH
LN_EPS = 1e-6
F32 = jnp.float32
BF16 = jnp.bfloat16


def dot(a, b, rhs_t=False):
    dims = (((1,), (1 if rhs_t else 0,)), ((), ()))
    return lax.dot_general(a, b, dims, preferred_element_type=F32)


def layer_norm(z, gain, bias):
    mean = jnp.mean(z, axis=-1, keepdims=True)
    centered = z - mean
    var = jnp.mean(centered * centered, axis=-1, keepdims=True)
    return centered * lax.rsqrt(var + LN_EPS) * gain + bias


def gelu_tanh(v):
    return 0.5 * v * (1.0 + jnp.tanh(math.sqrt(2.0 / math.pi) * (v + 0.044715 * (v * v * v))))


def kernel(cfg, img_hbm, wp_hbm, bp_hbm, pos_hbm, g1_hbm, b1_hbm, wqkv_hbm, bqkv_hbm, wo_hbm, bo_hbm, g2_hbm, c2_hbm,
           w1_hbm, bf1_hbm, w2_hbm, bf2_hbm, out_ref,
           img, wp, bp, pos, g1, b1, wqkv, bqkv, wo, bo, g2, c2, w1, bf1, w2, bf2,
           lhs, sel, x0h, x0r, bq, qb, kb, vb, ob, orx, acc,
           dsem, xs, xr, ks, kr, os_, or_):
    NZ, T, PL, C, D, H, HD, FF, NG = cfg
    me = lax.axis_index("sp")
    core = lax.rem(me, 2)
    z = lax.div(me, 2)
    partner = me + 1 - 2 * core
    ROWS = NZ * T

    def peer(t):
        return lax.rem(z + t + NZ, NZ) * 2 + core

    barrier = pltpu.get_barrier_semaphore()
    for t in range(1, NZ):
        pl.semaphore_signal(barrier, inc=1, device_id={"sp": peer(t)}, device_id_type=MESH)
    pl.semaphore_signal(barrier, inc=1, device_id={"sp": partner}, device_id_type=MESH)

    first = [(img_hbm, img), (wp_hbm.at[:, 0], wp.at[0]), (wp_hbm.at[:, 1], wp.at[1]), (wp_hbm.at[:, 2], wp.at[2]),
             (bp_hbm, bp), (pos_hbm, pos)]
    later = [(g1_hbm, g1), (b1_hbm, b1), (wqkv_hbm, wqkv), (bqkv_hbm, bqkv), (wo_hbm, wo), (bo_hbm, bo),
             (g2_hbm, g2), (c2_hbm, c2), (w1_hbm, w1), (bf1_hbm, bf1), (w2_hbm, w2), (bf2_hbm, bf2)]
    cps = [pltpu.make_async_copy(s, d, dsem.at[i]) for i, (s, d) in enumerate(first + later)]
    first_c, later_c = cps[:len(first)], cps[len(first):]
    for c in first_c:
        c.start()

    r = lax.broadcasted_iota(jnp.int32, (256, 256), 0)
    cc = lax.broadcasted_iota(jnp.int32, (256, 256), 1)
    same_q = lax.rem(r, 16) == lax.rem(cc, 16)
    for pp in range(PL // 2):
        hit = same_q & (lax.div(cc, 16) == 2 * pp + lax.div(r, 128))
        sel[pp * 256:(pp + 1) * 256, :] = jnp.where(hit, 1.0, 0.0).astype(BF16)

    first_c[0].wait()
    for c in later_c:
        c.start()

    m8 = lax.div(lax.broadcasted_iota(jnp.int32, (8, 128), 1), 16) == lax.broadcasted_iota(jnp.int32, (8, 128), 0)

    def spread(t, carry):
        b = lax.rem(z + t, NZ)
        for c in range(C):
            for p in range(PL):
                row = img[b, c, p:p + 1, :]
                lo = jnp.where(m8, jnp.broadcast_to(row[:, :128], (8, 128)), 0.0)
                hi = jnp.where(m8, jnp.broadcast_to(row[:, 128:], (8, 128)), 0.0)
                at = pl.multiple_of(c * ROWS + t * 16, 16)
                lhs[pl.ds(at, 16), p * 128:(p + 1) * 128] = jnp.concatenate([lo, hi], axis=0).astype(BF16)
        return carry

    lax.fori_loop(0, NZ, spread, 0)
    xsel = dot(lhs[...], sel[...]).astype(BF16)
    for c in first_c[1:]:
        c.wait()
    x0 = jnp.zeros((ROWS, D), F32)
    for c in range(C):
        x0 = x0 + dot(xsel[c * ROWS:(c + 1) * ROWS], wp[c].reshape(PL * 16, D))
    posb = jnp.broadcast_to(pos[...].astype(F32)[None], (NZ, T, D)).reshape(ROWS, D)
    x0 = (x0 + bp[...].reshape(1, D) + posb).astype(BF16)
    x0h[...] = x0
    x0r[0:T, :] = x0[0:T]

    pl.semaphore_wait(barrier, NZ)
    order = sorted(range(1, NZ), key=lambda t: -min(t, NZ - t))
    sends = []
    for t in order:
        cp = pltpu.make_async_remote_copy(src_ref=x0h.at[t * T:(t + 1) * T], dst_ref=x0r.at[t * T:(t + 1) * T],
                                          send_sem=xs.at[t], recv_sem=xr.at[t], device_id={"sp": peer(t)}, device_id_type=MESH)
        cp.start()
        sends.append(cp)

    for c in later_c[:4]:
        c.wait()
    for t3 in range(3):
        for h in range(H):
            bq[0:1, t3 * D + h * HD:t3 * D + (h + 1) * HD] = bqkv[t3, h:h + 1, :]

    for cp in sends:
        cp.wait_recv()

    y1 = layer_norm(x0r[...].astype(F32), g1[...].reshape(1, D), b1[...].reshape(1, D)).astype(BF16)
    GW = D // NG
    kv_c = []
    for g in range(NG):
        s = slice(g * GW, (g + 1) * GW)
        for j, buf in ((1, kb), (2, vb)):
            lo = j * D + g * GW
            buf[0:ROWS, s] = (dot(y1, wqkv[lo:lo + GW, :], rhs_t=True) + bq[0:1, lo:lo + GW]).astype(BF16)
        for j, buf in ((0, kb), (1, vb)):
            cp = pltpu.make_async_remote_copy(src_ref=buf.at[0:ROWS, s], dst_ref=buf.at[ROWS:2 * ROWS, s],
                                              send_sem=ks.at[2 * g + j], recv_sem=kr.at[2 * g + j],
                                              device_id={"sp": partner}, device_id_type=MESH)
            cp.start()
            kv_c.append(cp)
    for g in range(NG):
        s = slice(g * GW, (g + 1) * GW)
        qb[:, s] = (dot(y1, wqkv[g * GW:(g + 1) * GW, :], rhs_t=True) + bq[0:1, g * GW:(g + 1) * GW]).astype(BF16)

    left = lax.broadcasted_iota(jnp.int32, (ROWS, 128), 1) < HD
    osends = []
    scale = HD ** -0.5
    for g in range(NG):
        kv_c[2 * g].wait_recv()
        kv_c[2 * g + 1].wait_recv()
        for pr in range(GW // 128):
            s = slice(g * GW + pr * 128, g * GW + (pr + 1) * 128)
            q = qb[:, s]
            q2 = jnp.concatenate([jnp.where(left, q, jnp.zeros_like(q)), jnp.where(left, jnp.zeros_like(q), q)], axis=0)
            sc = dot(q2, kb[:, s], rhs_t=True) * scale
            e = jnp.exp(sc - jnp.max(sc, axis=-1, keepdims=True))
            p = (e * (1.0 / jnp.sum(e, axis=-1, keepdims=True))).astype(BF16)
            o2 = dot(p, vb[:, s])
            ob[:, s] = jnp.where(left, o2[:ROWS], o2[ROWS:]).astype(BF16)
        s = slice(g * GW, (g + 1) * GW)
        orx[0:T, s] = ob[0:T, s]
        for t in order:
            cp = pltpu.make_async_remote_copy(src_ref=ob.at[t * T:(t + 1) * T, s], dst_ref=orx.at[t * T:(t + 1) * T, s],
                                              send_sem=os_.at[g * NZ + t], recv_sem=or_.at[g * NZ + t],
                                              device_id={"sp": peer(-t)}, device_id_type=MESH)
            cp.start()
            osends.append(cp)

    for c in later_c[4:]:
        c.wait()
    res = x0h[...].astype(F32)
    n = len(order)
    for g in range(NG):
        for cp in osends[g * n:(g + 1) * n]:
            cp.wait_recv()
        s = slice(g * GW, (g + 1) * GW)
        res = res + dot(orx[:, s], wo[s, :])
    res = res + bo[...].reshape(1, D)
    y2 = layer_norm(res, g2[...].reshape(1, D), c2[...].reshape(1, D)).astype(BF16)
    acc[...] = res + bf2[...].reshape(1, D)
    FC = 768
    for f in range(FF // FC):
        s = slice(f * FC, (f + 1) * FC)
        hid = gelu_tanh(dot(y2, w1[:, s]) + bf1[...].reshape(1, FF)[:, s]).astype(BF16)
        acc[...] += dot(hid, w2[s, :])
    for t in range(NZ):
        out_ref[lax.rem(z + t, NZ)] = acc[t * T:(t + 1) * T, :].astype(BF16)

    for cp in sends + kv_c + osends:
        cp.wait_send()


def solution(mesh):
    def device_step(images, w_patch, b_patch, pos_embed, ln1_gain, ln1_bias, w_qkv, b_qkv, w_out, b_out, ln2_gain, ln2_bias, w_fc1, b_fc1, w_fc2, b_fc2):
        NB, PR, IW, C = images.shape
        PL, _, _, D = w_patch.shape
        H, HD = w_qkv.shape[2], w_qkv.shape[3]
        FF = w_fc1.shape[1]
        T = pos_embed.shape[0]
        NZ = mesh.shape["sp"] // 2
        assert NB == NZ and T == 16 and PL == 16 and IW == 256
        ROWS = NB * T
        NG = 3
        cfg = (NZ, T, PL, C, D, H, HD, FF, NG)
        vm = pltpu.VMEM
        dma = pltpu.SemaphoreType.DMA
        out = pl.pallas_call(
            functools.partial(kernel, cfg),
            out_shape=jax.ShapeDtypeStruct((NB, T, D), BF16),
            in_specs=[pl.BlockSpec(memory_space=pl.ANY)] * 16,
            out_specs=pl.BlockSpec(memory_space=pltpu.VMEM),
            scratch_shapes=[
                vm((NB, C, PL, IW), F32), vm((C, PL, 16, D), BF16), vm((D,), F32), vm((T, D), BF16),
                vm((D,), F32), vm((D,), F32), vm((3 * D, D), BF16), vm((3, H, HD), F32), vm((D, D), BF16), vm((D,), F32),
                vm((D,), F32), vm((D,), F32), vm((D, FF), BF16), vm((FF,), F32), vm((FF, D), BF16), vm((D,), F32),
                vm((C * ROWS, PL * 128), BF16), vm((PL * 128, 256), BF16), vm((ROWS, D), BF16), vm((ROWS, D), BF16),
                vm((1, 3 * D), F32), vm((ROWS, D), BF16), vm((2 * ROWS, D), BF16), vm((2 * ROWS, D), BF16),
                vm((ROWS, D), BF16), vm((ROWS, D), BF16), vm((ROWS, D), F32),
                dma((18,)), dma((NZ,)), dma((NZ,)), dma((2 * NG,)), dma((2 * NG,)), dma((NG * NZ,)), dma((NG * NZ,)),
            ],
            compiler_params=pltpu.CompilerParams(collective_id=0, has_side_effects=True, vmem_limit_bytes=60 * 1024 * 1024),
            name="siglip",
        )(
            images.transpose(0, 3, 1, 2),
            w_patch.transpose(0, 2, 1, 3),
            b_patch, pos_embed, ln1_gain, ln1_bias,
            w_qkv.transpose(1, 2, 3, 0).reshape(3 * D, D), b_qkv,
            w_out.reshape(D, D), b_out, ln2_gain, ln2_bias, w_fc1, b_fc1, w_fc2, b_fc2)
        return out

    in_specs = (P('dp', 'sp', None, None), P(), P(), P('sp', None), P(), P(), P(), P(), P(), P(), P(), P(), P(), P(), P(), P())
    return jax.shard_map(device_step, mesh=mesh, in_specs=in_specs, out_specs=P('dp', 'sp', None), check_vma=False)
```

time: 174 us -> 31.1 us (0.18)
  waiting for transfers between devices: 81.3 us -> 0 us
  matrix products: 41.6 us -> 0 us
  local copies, waits for them, and re-layouts: 33.1 us -> 1.62 us
  Pallas kernels: 0 us -> 29 us
  between operations: 13.6 us -> 0.01 us
  other arithmetic: 3.58 us -> 0 us
    all_gather x1 -> x0, waiting for transfers between devices: 81.2 us -> none  [device_step(): key_value = lax.all_gather(qkv_proj[:, :, 1:], 'sp', axis=1, tiled=True)]
    dot_general x12 -> x0, matrix products: 30.7 us -> none  [the longest x8 17.6 us: one_group(): jnp.einsum('hqk,khe->qhe', att_weights, v_img, preferred_element_type=jnp...]
    pallas_call x0 -> x1, Pallas kernels: none -> 29 us  [device_step(): pl.pallas_call(functools.partial(kernel, cfg), out_shape=jax.ShapeDtypeSt...]
    squeeze x2 -> x0, local copies, waits for them, and re-layouts: 13.8 us -> none  [device_step(): attended = attend(qkv_proj[:, :, 0], key_value[:, :, 0], key_value[:, :, 1])]
    while x2 -> x0, local copies, waits for them, and re-layouts: 13.5 us -> none  [attend(): return lax.map(one_image, (queries, keys_all, values_all))]
    sub x8 -> x0, matrix products: 10.8 us -> none  [one_group(): att_weights = jax.nn.softmax(scores, axis=-1).astype(jnp.bfloat16)]
    convert_element_type x2 -> x0, other arithmetic: 3.21 us -> none  [the longest x1 1.7 us: embed_tokens(): images.astype(jnp.bfloat16)]
    reshape x1 -> x0, local copies, waits for them, and re-layouts: 2.94 us -> none
  transfers between devices with their start and end apart: 1 -> 0, of which waited for: 1 -> 0; matrix products, arithmetic and copies ran while one was open for 1% -> 0% of each run, Pallas kernels for 0% -> 0%
where the time goes in v1:
time: 31.1 us; the launch traced here: 30.6 us
  Pallas kernels  29 us (93%)
  local copies, waits for them, and re-layouts  1.62 us (5%)
    pallas_call x1, Pallas kernels, device_step(): pl.pallas_call(functools.partial(kernel, cfg), out_shape=jax.ShapeDtypeSt...  29 us
    unnamed x1, local copies, waits for them, and re-layouts  1.62 us

profile of v1, /device:TPU:21, one launch (start us, length us, event | category | flops | bytes accessed | tf_op | source)
XLA Modules:
  0.0 30.6 jit_solution(10509248392958211309)
XLA Ops:
  0.0 29.0 %siglip.1 = bf16[8,16,768]{2,1,0:T(8,128)(2,1)} custom-call(f32[8,3,16,256]{3,2,1,0:T(8,128)} %bitcast.9, bf16[16,3,16,768]{3,2,1,0:T(8,128)(2,1)} %bitcast.7, f32[768]{0:T(1024)} %bp_hbm.1, bf16[16,768]{1,0:T(8,128)(2,1)} %pos_hbm.1, f32[768]{0:T(1024)} %g1_hbm.1, f32[768]{0:T(1024)} %b1_hbm.1, bf16[2304,768]{1,0:T(8,128)(2,1)} %bitcast.6, ...), custom_call_target="tpu_custom_call" | custom-call | tf_op jit(solution)/shard_map/siglip/pallas_call | solution.py:196
  29.0 1.6 %copy.18 = bf16[8,16,768]{2,1,0:T(8,128)(2,1)} copy(bf16[8,16,768]{2,1,0:T(8,128)(2,1)} %siglip.1) | data formatting | bytes 393216

commit v2 on v1

v2 whole, which is shorter than its diff:
```python
import functools
import math

import jax
import jax.numpy as jnp
from jax import lax
from jax.experimental import pallas as pl
from jax.experimental.pallas import tpu as pltpu
from jax.sharding import PartitionSpec as P

MESH = pl.DeviceIdType.MESH
LN_EPS = 1e-6
F32 = jnp.float32
BF16 = jnp.bfloat16


def dot(a, b, rhs_t=False):
    dims = (((1,), (1 if rhs_t else 0,)), ((), ()))
    return lax.dot_general(a, b, dims, preferred_element_type=F32)


def layer_norm(z, gain, bias):
    mean = jnp.mean(z, axis=-1, keepdims=True)
    centered = z - mean
    var = jnp.mean(centered * centered, axis=-1, keepdims=True)
    return centered * lax.rsqrt(var + LN_EPS) * gain + bias


def gelu_tanh(v):
    return 0.5 * v * (1.0 + jnp.tanh(math.sqrt(2.0 / math.pi) * (v + 0.044715 * (v * v * v))))


def kernel(cfg, img_hbm, wp_hbm, bp_hbm, pos_hbm, g1_hbm, b1_hbm, wqkv_hbm, bqkv_hbm, wo_hbm, bo_hbm, g2_hbm, c2_hbm,
           w1_hbm, bf1_hbm, w2_hbm, bf2_hbm, out_ref,
           img, wp, bp, pos, g1, b1, wqkv, bqkv, wo, bo, g2, c2, w1, bf1, w2, bf2,
           lhs, sel, x0h, yh, yr, wt, bq, qb, kvb, ob, orx, acc,
           dsem, isem, xs, xr, ks, kr, os_, or_):
    NZ, T, PL, C, D, H, HD, FF = cfg
    NP = D // 128
    me = lax.axis_index("sp")
    core = lax.rem(me, 2)
    z = lax.div(me, 2)
    partner = me + 1 - 2 * core
    ROWS = NZ * T

    def peer(t):
        return lax.rem(z + t + NZ, NZ) * 2 + core

    def remote(src, dst, ssem, rsem, to):
        return pltpu.make_async_remote_copy(src_ref=src, dst_ref=dst, send_sem=ssem, recv_sem=rsem,
                                            device_id={"sp": to}, device_id_type=MESH)

    barrier = pltpu.get_barrier_semaphore()
    for t in range(1, NZ):
        pl.semaphore_signal(barrier, inc=1, device_id={"sp": peer(t)}, device_id_type=MESH)
    pl.semaphore_signal(barrier, inc=1, device_id={"sp": partner}, device_id_type=MESH)

    order = sorted(range(1, NZ), key=lambda t: -min(t, NZ - t)) + [0]
    img_c = [pltpu.make_async_copy(img_hbm.at[lax.rem(z + t, NZ)], img.at[i], isem.at[i]) for i, t in enumerate(order)]
    first = [(wp_hbm.at[:, c], wp.at[c]) for c in range(C)] + [(bp_hbm, bp), (pos_hbm, pos), (g1_hbm, g1), (b1_hbm, b1)]
    later = [(wqkv_hbm, wqkv), (bqkv_hbm, bqkv), (wo_hbm, wo), (bo_hbm, bo),
             (g2_hbm, g2), (c2_hbm, c2), (w1_hbm, w1), (bf1_hbm, bf1), (w2_hbm, w2), (bf2_hbm, bf2)]
    cps = [pltpu.make_async_copy(s, d, dsem.at[i]) for i, (s, d) in enumerate(first + later)]
    first_c, later_c = cps[:len(first)], cps[len(first):]
    for c in img_c + first_c:
        c.start()

    r = lax.broadcasted_iota(jnp.int32, (256, 256), 0)
    cc = lax.broadcasted_iota(jnp.int32, (256, 256), 1)
    same_q = lax.rem(r, 16) == lax.rem(cc, 16)
    for pp in range(PL // 2):
        hit = same_q & (lax.div(cc, 16) == 2 * pp + lax.div(r, 128))
        sel[pp * 256:(pp + 1) * 256, :] = jnp.where(hit, 1.0, 0.0).astype(BF16)
    m8 = lax.div(lax.broadcasted_iota(jnp.int32, (8, 128), 1), 16) == lax.broadcasted_iota(jnp.int32, (8, 128), 0)
    GI = 2
    CH = 4
    CR = CH * T

    def spread(k):
        for i in range(CH):
            for c in range(C):
                for p in range(PL):
                    row = img[k * CH + i, c, p:p + 1, :]
                    lo = jnp.where(m8, jnp.broadcast_to(row[:, :128], (8, 128)), 0.0)
                    hi = jnp.where(m8, jnp.broadcast_to(row[:, 128:], (8, 128)), 0.0)
                    at = (((k * CH + i) // GI * C + c) * GI + i % GI) * T
                    lhs[at:at + T, p * 128:(p + 1) * 128] = jnp.concatenate([lo, hi], axis=0).astype(BF16)

    sends = []
    for k in range(NZ // CH):
        for c in img_c[k * CH:(k + 1) * CH]:
            c.wait()
        spread(k)
        xcat = []
        for u in range(CH // GI):
            at = (k * CH // GI + u) * C * GI * T
            xsel = dot(lhs[at:at + C * GI * T, :], sel[...]).astype(BF16)
            xcat.append(jnp.concatenate([xsel[c * GI * T:(c + 1) * GI * T] for c in range(C)], axis=1))
        if k == 0:
            for c in first_c:
                c.wait()
        x0 = dot(jnp.concatenate(xcat, axis=0), wp[...].reshape(C * PL * 16, D))
        posb = jnp.broadcast_to(pos[...].astype(F32)[None], (CH, T, D)).reshape(CR, D)
        x0 = (x0 + bp[...].reshape(1, D) + posb).astype(BF16)
        x0h[k * CR:(k + 1) * CR, :] = x0
        y1 = layer_norm(x0.astype(F32), g1[...].reshape(1, D), b1[...].reshape(1, D)).astype(BF16)
        yh[k * CR:(k + 1) * CR, :] = y1
        if k == NZ // CH - 1:
            yr[ROWS - T:ROWS, :] = y1[CR - T:]
        if k == 0:
            for c in later_c:
                c.start()
            pl.semaphore_wait(barrier, NZ)
        for i in range(k * CH, min((k + 1) * CH, NZ - 1)):
            cp = remote(yh.at[i * T:(i + 1) * T], yr.at[i * T:(i + 1) * T], xs.at[i], xr.at[i], peer(order[i]))
            cp.start()
            sends.append(cp)

    for c in later_c[:2]:
        c.wait()
    GW = 256
    NG = D // GW
    for n in range(3 * NP):
        j, pr = divmod(n, NP)
        to = n * 128 if j == 0 else D + pr // 2 * 2 * GW + (j - 1) * GW + pr % 2 * 128
        wt[:, to:to + 128] = wqkv[n * 128:(n + 1) * 128, :].T
        for h in range(2):
            bq[0:1, to + h * HD:to + (h + 1) * HD] = bqkv[j, 2 * pr + h:2 * pr + h + 1, :]

    for cp in sends:
        cp.wait_recv()

    y1 = yr[...]
    kv_c = []
    for g in range(NG):
        lo = D + g * 2 * GW
        sl = slice(g * 2 * GW, (g + 1) * 2 * GW)
        kvb[0:ROWS, sl] = (dot(y1, wt[:, lo:lo + 2 * GW]) + bq[0:1, lo:lo + 2 * GW]).astype(BF16)
        cp = remote(kvb.at[0:ROWS, sl], kvb.at[ROWS:2 * ROWS, sl], ks.at[g], kr.at[g], partner)
        cp.start()
        kv_c.append(cp)
    qb[...] = (dot(y1, wt[:, 0:D]) + bq[0:1, 0:D]).astype(BF16)

    left = lax.broadcasted_iota(jnp.int32, (ROWS, 128), 1) < HD
    osends = []
    scale = HD ** -0.5
    NF = 3
    for g in range(NG):
        kv_c[g].wait_recv()
        for u in range(GW // 128):
            s = slice(g * GW + u * 128, g * GW + (u + 1) * 128)
            kc = g * 2 * GW + u * 128
            q = qb[:, s]
            q2 = jnp.concatenate([jnp.where(left, q, jnp.zeros_like(q)), jnp.where(left, jnp.zeros_like(q), q)], axis=0)
            sc = dot(q2, kvb[:, kc:kc + 128], rhs_t=True) * scale
            e = jnp.exp(sc - jnp.max(sc, axis=-1, keepdims=True))
            p = (e * (1.0 / jnp.sum(e, axis=-1, keepdims=True))).astype(BF16)
            o2 = dot(p, kvb[:, kc + GW:kc + GW + 128])
            o = jnp.where(left, o2[:ROWS], o2[ROWS:]).astype(BF16)
            ob[:, s] = o
            orx[ROWS - T:ROWS, s] = o[ROWS - T:]
        s = slice(g * GW, (g + 1) * GW)
        for i in range(NF):
            n = g * NF + i
            cp = remote(ob.at[i * T:(i + 1) * T, s], orx.at[i * T:(i + 1) * T, s], os_.at[n], or_.at[n], peer(-order[i]))
            cp.start()
            osends.append(cp)
    for i in range(NF, NZ - 1):
        n = NG * NF + i - NF
        cp = remote(ob.at[i * T:(i + 1) * T], orx.at[i * T:(i + 1) * T], os_.at[n], or_.at[n], peer(-order[i]))
        cp.start()
        osends.append(cp)

    for c in later_c[2:]:
        c.wait()
    for cp in osends:
        cp.wait_recv()
    acc[...] = x0h[...].astype(F32) + bo[...].reshape(1, D) + dot(orx[...], wo[...])
    res = acc[...]
    y2 = layer_norm(res, g2[...].reshape(1, D), c2[...].reshape(1, D)).astype(BF16)
    acc[...] = res + bf2[...].reshape(1, D)
    FC = 768
    for f in range(FF // FC):
        s = slice(f * FC, (f + 1) * FC)
        hid = gelu_tanh(dot(y2, w1[:, s]) + bf1[...].reshape(1, FF)[:, s]).astype(BF16)
        acc[...] += dot(hid, w2[s, :])
    for i in range(NZ):
        out_ref[lax.rem(z + order[i], NZ)] = acc[i * T:(i + 1) * T, :].astype(BF16)

    for cp in sends + kv_c + osends:
        cp.wait_send()


def solution(mesh):
    def device_step(images, w_patch, b_patch, pos_embed, ln1_gain, ln1_bias, w_qkv, b_qkv, w_out, b_out, ln2_gain, ln2_bias, w_fc1, b_fc1, w_fc2, b_fc2):
        NB, PR, IW, C = images.shape
        PL, _, _, D = w_patch.shape
        H, HD = w_qkv.shape[2], w_qkv.shape[3]
        FF = w_fc1.shape[1]
        T = pos_embed.shape[0]
        NZ = mesh.shape["sp"] // 2
        assert NB == NZ and T == 16 and PL == 16 and IW == 256 and HD == 64
        ROWS = NB * T
        NP = D // 128
        cfg = (NZ, T, PL, C, D, H, HD, FF)
        vm = pltpu.VMEM
        dma = pltpu.SemaphoreType.DMA
        operands = (
            images.transpose(0, 3, 1, 2), w_patch.transpose(0, 2, 1, 3), b_patch, pos_embed, ln1_gain, ln1_bias,
            w_qkv.transpose(1, 2, 3, 0).reshape(3 * D, D), b_qkv, w_out.reshape(D, D), b_out, ln2_gain, ln2_bias,
            w_fc1, b_fc1, w_fc2, b_fc2)
        return pl.pallas_call(
            functools.partial(kernel, cfg),
            out_shape=jax.ShapeDtypeStruct((NB, T, D), BF16),
            in_specs=[pl.BlockSpec(memory_space=pltpu.HBM)] * len(operands),
            out_specs=pl.BlockSpec(memory_space=pltpu.VMEM),
            scratch_shapes=[
                vm((NB, C, PL, IW), F32), vm((C, PL, 16, D), BF16), vm((D,), F32), vm((T, D), BF16),
                vm((D,), F32), vm((D,), F32), vm((3 * D, D), BF16), vm((3, H, HD), F32), vm((D, D), BF16), vm((D,), F32),
                vm((D,), F32), vm((D,), F32), vm((D, FF), BF16), vm((FF,), F32), vm((FF, D), BF16), vm((D,), F32),
                vm((C * ROWS, PL * 128), BF16), vm((PL * 128, 256), BF16), vm((ROWS, D), BF16), vm((ROWS, D), BF16), vm((ROWS, D), BF16),
                vm((D, 3 * D), BF16), vm((1, 3 * D), F32), vm((ROWS, D), BF16), vm((2 * ROWS, 2 * D), BF16),
                vm((ROWS, D), BF16), vm((ROWS, D), BF16), vm((ROWS, D), F32),
                dma((17,)), dma((NZ,)), dma((NZ,)), dma((NZ,)), dma((3,)), dma((3,)), dma((3 * NZ,)), dma((3 * NZ,)),
            ],
            compiler_params=pltpu.CompilerParams(collective_id=0, has_side_effects=True, vmem_limit_bytes=40 * 1024 * 1024),
            name="siglip",
        )(*[pltpu.with_memory_space_constraint(a, pltpu.HBM) for a in operands])

    in_specs = (P('dp', 'sp', None, None), P(), P(), P('sp', None), P(), P(), P(), P(), P(), P(), P(), P(), P(), P(), P(), P())
    return jax.shard_map(device_step, mesh=mesh, in_specs=in_specs, out_specs=P('dp', 'sp', None), check_vma=False)
```

time: 31.1 us -> 28.9 us (0.929); the launches traced: 30.6 us -> 28.9 us
  local copies, waits for them, and re-layouts: 1.62 us -> 0.68 us
  Pallas kernels: 29 us -> 28.2 us
    unnamed x1, local copies, waits for them, and re-layouts: 1.62 us -> 0.68 us
    pallas_call x1, Pallas kernels: 29 us -> 28.2 us  [device_step(): pl.pallas_call(functools.partial(kernel, cfg), out_shape=jax.ShapeDtypeSt...]
where the time goes in v2:
time: 28.9 us
  Pallas kernels  28.2 us (98%)
  local copies, waits for them, and re-layouts  0.68 us (2%)
    pallas_call x1, Pallas kernels, device_step(): pl.pallas_call(functools.partial(kernel, cfg), out_shape=jax.ShapeDtypeSt...  28.2 us
    unnamed x1, local copies, waits for them, and re-layouts  0.68 us

profile of v2, /device:TPU:21, one launch (start us, length us, event | category | flops | bytes accessed | tf_op | source)
XLA Modules:
  0.0 28.9 jit_solution(10715201351611340747)
XLA Ops:
  0.0 28.2 %siglip.1 = bf16[8,16,768]{2,1,0:T(8,128)(2,1)S(1)} custom-call(f32[8,3,16,256]{3,2,1,0:T(8,128)} %bitcast.9, bf16[16,3,16,768]{3,2,1,0:T(8,128)(2,1)} %bitcast.7, f32[768]{0:T(1024)} %bp_hbm.1, bf16[16,768]{1,0:T(8,128)(2,1)} %pos_hbm.1, f32[768]{0:T(1024)} %g1_hbm.1, f32[768]{0:T(1024)} %b1_hbm.1, bf16[2304,768]{1,0:T(8,128)(2,1)} %bitcast.6, ...), custom_call_target="tpu_custom_call" | custom-call | tf_op jit(solution)/shard_map/siglip/pallas_call | solution.py:212
  28.2 0.7 %copy.18 = bf16[8,16,768]{2,1,0:T(8,128)(2,1)} copy(bf16[8,16,768]{2,1,0:T(8,128)(2,1)S(1)} %siglip.1) | data formatting | bytes 393216
